TPU v7x, 32 devices: a whole 2x2x4 slice. The times are simulated.
32 devices in a mesh: dp: 8 (over z, x), ctx: 4 (over y, core).
Axes of the slice: x: 2, y: 2, z: 4, core: 2. Of those that a mesh axis runs over, the one named last changes fastest.
Arguments:
- tokens: bfloat16 [8192, 1536], P(('dp', 'ctx')), may hold values from -6 to 6
- norm_attn: float32 [1536], P(('dp', 'ctx')), may hold values from 0.5 to 1.5
- w_qkv: bfloat16 [3072, 1536], P(('dp', 'ctx')), may hold values from -1 to 1
- w_out: bfloat16 [1536, 1536], P(('dp', 'ctx')), may hold values from -0.875 to 0.875
- norm_mlp: float32 [1536], P(('dp', 'ctx')), may hold values from 0.5 to 1.5
- w_gate_up: bfloat16 [8192, 1536], P(('dp', 'ctx')), may hold values from -0.15625 to 0.15625
- w_down: bfloat16 [1536, 4096], P(('dp', 'ctx')), may hold values from -0.09375 to 0.09375
- cotangent: bfloat16 [8192, 1536], P(('dp', 'ctx')), may hold values from -6 to 6
- seq_lengths: int32 [8, 2], P('dp'), may hold values from 1 to 768, 1024 in all within a row
- block_slot: int32 [8, 8], P('dp'), may hold values from 0 to 7, each once within a row
Outputs:
- result: bfloat16 [8192, 1536], P(('dp', 'ctx'))
- grad_input: float32 [8192, 1536], P(('dp', 'ctx'))
- grad_norm_attn: float32 [1536], P(('dp', 'ctx'))
- grad_qkv: float32 [3072, 1536], P(('dp', 'ctx'))
- grad_out: float32 [1536, 1536], P(('dp', 'ctx'))
- grad_norm_mlp: float32 [1536], P(('dp', 'ctx'))
- grad_gate_up: float32 [8192, 1536], P(('dp', 'ctx'))
- grad_down: float32 [1536, 4096], P(('dp', 'ctx'))
Inputs may be any that keep to these rules, and one draw needn't show every extreme that they name: `seq_lengths`: each row sums to 1024. `block_slot`: each row names every number once; ctx device c of group g holds the blocks of positions c * 2 to (c + 1) * 2 - 1 of that row.
All inputs are finite; a program needn't handle non-finite values.
Results may differ from a plain program's by a relative error of at most 0.025.
Values may be sent and summed in bfloat16 or wider, within the bound.
A program may use at most 320 MiB of HBM per device.

v0:
```python
import math
import jax
import jax.numpy as jnp
from jax import lax
from jax.sharding import PartitionSpec as P

QUERY_HEADS = 16
KEY_VALUE_HEADS = 8
HEAD_SIZE = 96
FF = 4096
BLK = 128
QUERY_FEATURES = 1536
KEY_FEATURES = 768
EPSILON = 1e-05
THETA = 100000.0
MASK_FILL = -1e30


def rope_tables(rope_pos):
    half_dim = HEAD_SIZE // 2
    exponent = jnp.arange(half_dim, dtype=jnp.float32) * (2.0 / HEAD_SIZE)
    frequency = jnp.power(jnp.float32(THETA), -exponent)
    angles = rope_pos.astype(jnp.float32)[:, None] * frequency[None, :]
    return (jnp.cos(angles)[:, None, :], jnp.sin(angles)[:, None, :])


def apply_rotation(values, cosine_table, sine_values):
    half_dim = HEAD_SIZE // 2
    first_half = values[..., :half_dim]
    second_half = values[..., half_dim:]
    return jnp.concatenate(
        [
            first_half * cosine_table - second_half * sine_values,
            second_half * cosine_table + first_half * sine_values,
        ],
        -1,
    )


def rotate_back(gradient, cosine_table, sine_values):
    half_dim = HEAD_SIZE // 2
    first_half = gradient[..., :half_dim]
    second_half = gradient[..., half_dim:]
    return jnp.concatenate(
        [
            first_half * cosine_table + second_half * sine_values,
            second_half * cosine_table - first_half * sine_values,
        ],
        -1,
    )


def positions(lengths, slot_table, first_row, count_of_rows):
    row_index = first_row + jnp.arange(count_of_rows, dtype=jnp.int32)
    block_index = row_index // BLK
    lookup = jnp.arange(slot_table.shape[0], dtype=jnp.int32)
    slot_of = jnp.sum(jnp.where(block_index[:, None] == lookup[None, :], slot_table[None, :], 0), 1)
    stream = slot_of * BLK + row_index % BLK
    seq_ends = jnp.cumsum(lengths)
    passed = stream[:, None] >= seq_ends[None, :]
    segment = jnp.sum(passed.astype(jnp.int32), 1)
    offset = jnp.sum(jnp.where(passed, seq_ends[None, :], 0), 1)
    return (stream, segment, stream - offset)


def norm_back(grad_normed, gain, source, scale):
    weighted = grad_normed * gain
    return scale * weighted - source * scale**3 * jnp.mean(weighted * source, -1, keepdims=True)


def full_product(left_side, whole_weight):
    return jnp.dot(left_side, whole_weight.T, preferred_element_type=jnp.float32)


def full_back(grad_side, whole_weight):
    return jnp.dot(grad_side, whole_weight, preferred_element_type=jnp.float32)


def owned_three(first_part, second_part, third_part):
    return (
        lax.psum_scatter(first_part, ("dp", "ctx"), scatter_dimension=0, tiled=True),
        lax.psum_scatter(second_part, ("dp", "ctx"), scatter_dimension=0, tiled=True),
        lax.psum_scatter(third_part, ("dp", "ctx"), scatter_dimension=0, tiled=True),
    )


def shards(
    tokens, norm_attn, w_qkv, w_out, norm_mlp, w_gate_up, w_down, cotangent, seq_lengths, block_slot
):
    count_of_rows = tokens.shape[0]
    ctx_place = lax.axis_index("ctx")
    lengths = seq_lengths[0]
    slot_table = block_slot[0]
    heads_ratio = QUERY_HEADS // KEY_VALUE_HEADS
    score_scale = 1.0 / math.sqrt(HEAD_SIZE)
    stream, segment, rope_pos = positions(
        lengths, slot_table, ctx_place * count_of_rows, count_of_rows
    )
    cosine_table, sine_values = rope_tables(rope_pos)
    gain_one, gain_two = (
        lax.all_gather(norm_attn, ("dp", "ctx"), axis=0, tiled=True),
        lax.all_gather(norm_mlp, ("dp", "ctx"), axis=0, tiled=True),
    )
    qkv_full, out_full = (
        lax.all_gather(w_qkv, ("dp", "ctx"), axis=0, tiled=True),
        lax.all_gather(w_out, ("dp", "ctx"), axis=0, tiled=True),
    )
    source = tokens.astype(jnp.float32)
    scale_one = lax.rsqrt(jnp.mean(source * source, -1, keepdims=True) + EPSILON)
    normed_one = (source * scale_one * gain_one).astype(jnp.bfloat16)
    projected_output = full_product(normed_one, qkv_full)
    query_rows = apply_rotation(
        projected_output[:, :QUERY_FEATURES].reshape(count_of_rows, QUERY_HEADS, HEAD_SIZE),
        cosine_table,
        sine_values,
    ).astype(jnp.bfloat16)
    keys_mine = apply_rotation(
        projected_output[:, QUERY_FEATURES : QUERY_FEATURES + KEY_FEATURES].reshape(
            count_of_rows, KEY_VALUE_HEADS, HEAD_SIZE
        ),
        cosine_table,
        sine_values,
    ).astype(jnp.bfloat16)
    values_mine = projected_output[:, QUERY_FEATURES + KEY_FEATURES :].astype(jnp.bfloat16)
    grouped_queries = query_rows.reshape(count_of_rows, KEY_VALUE_HEADS, heads_ratio, HEAD_SIZE)
    key_value = jnp.concatenate([keys_mine.reshape(count_of_rows, KEY_FEATURES), values_mine], 1)

    def masked(block_portion, start_row):
        portion_rows = block_portion.shape[0]
        key_stream, key_segment, unused = positions(lengths, slot_table, start_row, portion_rows)
        key_portion = block_portion[:, :KEY_FEATURES].reshape(
            portion_rows, KEY_VALUE_HEADS, HEAD_SIZE
        )
        value_portion = block_portion[:, KEY_FEATURES:].reshape(
            portion_rows, KEY_VALUE_HEADS, HEAD_SIZE
        )
        scores = (
            jnp.einsum(
                "rgjd,ngd->gjrn", grouped_queries, key_portion, preferred_element_type=jnp.float32
            )
            * score_scale
        )
        allowed = (
            (segment[:, None] == key_segment[None, :]) & (key_stream[None, :] <= stream[:, None])
        )[None, None]
        return (jnp.where(allowed, scores, MASK_FILL), allowed, key_portion, value_portion)

    highest_score = jnp.full((KEY_VALUE_HEADS, heads_ratio, count_of_rows), MASK_FILL, jnp.float32)
    scores, allowed, key_portion, value_portion = masked(
        lax.all_gather(key_value, "ctx", axis=0, tiled=True), jnp.int32(0)
    )
    new_high = jnp.maximum(highest_score, jnp.max(scores, -1))
    weights = jnp.where(allowed, jnp.exp(scores - new_high[..., None]), 0.0)
    weight_sum = jnp.sum(weights, -1)
    gained = jnp.einsum(
        "gjrn,ngd->rgjd",
        weights.astype(jnp.bfloat16),
        value_portion,
        preferred_element_type=jnp.float32,
    )
    accumulated = gained
    highest_score, weight_sum, accumulated = (new_high, weight_sum, accumulated)
    log_total = highest_score + jnp.log(weight_sum)
    attention_output = (
        (accumulated / jnp.transpose(weight_sum, (2, 0, 1))[..., None])
        .astype(jnp.bfloat16)
        .reshape(count_of_rows, QUERY_FEATURES)
    )
    residual = source + full_product(attention_output, out_full)
    scale_two = lax.rsqrt(jnp.mean(residual * residual, -1, keepdims=True) + EPSILON)
    normed_two = (residual * scale_two * gain_two).astype(jnp.bfloat16)
    gate_up_full, down_full = (
        lax.all_gather(w_gate_up, ("dp", "ctx"), axis=0, tiled=True),
        lax.all_gather(w_down, ("dp", "ctx"), axis=0, tiled=True),
    )
    gate_up = full_product(normed_two, gate_up_full)
    gate_part = gate_up[:, :FF]
    up_part = gate_up[:, FF:]
    sigmoid = jax.nn.sigmoid(gate_part)
    hidden = (gate_part * sigmoid * up_part).astype(jnp.bfloat16)
    mlp_term = full_product(hidden, down_full)
    result = (residual + mlp_term).astype(jnp.bfloat16)
    gate_up_full, down_full = (
        lax.all_gather(w_gate_up, ("dp", "ctx"), axis=0, tiled=True),
        lax.all_gather(w_down, ("dp", "ctx"), axis=0, tiled=True),
    )
    grad_hidden = full_back(cotangent, down_full)
    grad_down = jnp.dot(cotangent.T, hidden, preferred_element_type=jnp.float32)
    grad_gate = grad_hidden * up_part * sigmoid * (1.0 + gate_part * (1.0 - sigmoid))
    grad_upper = grad_hidden * gate_part * sigmoid
    grad_gu = jnp.concatenate([grad_gate, grad_upper], 1).astype(jnp.bfloat16)
    grad_normed_two = full_back(grad_gu, gate_up_full)
    grad_w_gate_up = jnp.dot(grad_gu.T, normed_two, preferred_element_type=jnp.float32)
    grad_gain_two = jnp.sum(grad_normed_two * residual * scale_two, 0)
    mlp_owned = owned_three(grad_gain_two, grad_w_gate_up, grad_down)
    grad_residual = cotangent.astype(jnp.float32) + norm_back(
        grad_normed_two, gain_two, residual, scale_two
    )
    grad_res_bf = grad_residual.astype(jnp.bfloat16)
    qkv_full, out_full = (
        lax.all_gather(w_qkv, ("dp", "ctx"), axis=0, tiled=True),
        lax.all_gather(w_out, ("dp", "ctx"), axis=0, tiled=True),
    )
    attention_gradient = full_back(grad_res_bf, out_full).astype(jnp.bfloat16)
    grad_w_out = jnp.dot(grad_res_bf.T, attention_output, preferred_element_type=jnp.float32)
    keys_values_all = lax.all_gather(key_value, "ctx", axis=0, tiled=True)
    grouped_gradient = attention_gradient.reshape(
        count_of_rows, KEY_VALUE_HEADS, heads_ratio, HEAD_SIZE
    )
    attention_grouped = attention_output.reshape(
        count_of_rows, KEY_VALUE_HEADS, heads_ratio, HEAD_SIZE
    )
    row_delta = jnp.transpose(
        jnp.sum(grouped_gradient.astype(jnp.float32) * attention_grouped.astype(jnp.float32), -1),
        (1, 2, 0),
    )
    grouped_rows = keys_values_all.shape[0]
    block_rows = min(512, grouped_rows)
    block_count = grouped_rows // block_rows

    def key_block(grad_queries, which_block):
        start_row = which_block * block_rows
        block_portion = lax.dynamic_slice_in_dim(keys_values_all, start_row, block_rows, 0)
        scores, allowed, key_portion, value_portion = masked(block_portion, start_row)
        weights = jnp.where(allowed, jnp.exp(scores - log_total[..., None]), 0.0)
        grad_values = jnp.einsum(
            "gjrn,rgjd->ngd",
            weights.astype(jnp.bfloat16),
            grouped_gradient,
            preferred_element_type=jnp.float32,
        )
        grad_weights = jnp.einsum(
            "rgjd,ngd->gjrn", grouped_gradient, value_portion, preferred_element_type=jnp.float32
        )
        grad_scores = (weights * (grad_weights - row_delta[..., None])).astype(jnp.bfloat16)
        grad_queries = (
            grad_queries
            + jnp.einsum(
                "gjrn,ngd->rgjd", grad_scores, key_portion, preferred_element_type=jnp.float32
            )
            * score_scale
        )
        grad_keys = (
            jnp.einsum(
                "gjrn,rgjd->ngd", grad_scores, grouped_queries, preferred_element_type=jnp.float32
            )
            * score_scale
        )
        return (
            grad_queries,
            jnp.concatenate(
                [
                    grad_keys.reshape(block_rows, KEY_FEATURES),
                    grad_values.reshape(block_rows, KEY_FEATURES),
                ],
                1,
            ),
        )

    grad_queries, key_terms = lax.scan(
        key_block,
        jnp.zeros((count_of_rows, KEY_VALUE_HEADS, heads_ratio, HEAD_SIZE), jnp.float32),
        jnp.arange(block_count, dtype=jnp.int32),
    )
    key_value_gradient = lax.psum_scatter(
        key_terms.reshape(grouped_rows, 2 * KEY_FEATURES).astype(jnp.bfloat16),
        "ctx",
        scatter_dimension=0,
        tiled=True,
    ).astype(jnp.float32)
    grad_queries = rotate_back(
        grad_queries.reshape(count_of_rows, QUERY_HEADS, HEAD_SIZE), cosine_table, sine_values
    ).reshape(count_of_rows, QUERY_FEATURES)
    grad_keys = rotate_back(
        key_value_gradient[:, :KEY_FEATURES].reshape(count_of_rows, KEY_VALUE_HEADS, HEAD_SIZE),
        cosine_table,
        sine_values,
    ).reshape(count_of_rows, KEY_FEATURES)
    grad_projected = jnp.concatenate(
        [grad_queries, grad_keys, key_value_gradient[:, KEY_FEATURES:]], 1
    ).astype(jnp.bfloat16)
    grad_normed_one = full_back(grad_projected, qkv_full)
    grad_w_qkv = jnp.dot(grad_projected.T, normed_one, preferred_element_type=jnp.float32)
    grad_gain_one = jnp.sum(grad_normed_one * source * scale_one, 0)
    grad_tokens = grad_residual + norm_back(grad_normed_one, gain_one, source, scale_one)
    attn_owned = owned_three(grad_gain_one, grad_w_qkv, grad_w_out)
    return (
        result,
        grad_tokens,
        attn_owned[0],
        attn_owned[1],
        attn_owned[2],
        mlp_owned[0],
        mlp_owned[1],
        mlp_owned[2],
    )


def solution(mesh):
    return jax.shard_map(
        shards,
        mesh=mesh,
        in_specs=(
            P(("dp", "ctx"), None),
            P(("dp", "ctx")),
            P(("dp", "ctx"), None),
            P(("dp", "ctx"), None),
            P(("dp", "ctx")),
            P(("dp", "ctx"), None),
            P(("dp", "ctx"), None),
            P(("dp", "ctx"), None),
            P("dp", None),
            P("dp", None),
        ),
        out_specs=(
            P(("dp", "ctx"), None),
            P(("dp", "ctx"), None),
            P(("dp", "ctx")),
            P(("dp", "ctx"), None),
            P(("dp", "ctx"), None),
            P(("dp", "ctx")),
            P(("dp", "ctx"), None),
            P(("dp", "ctx"), None),
        ),
        check_vma=False,
    )
```

profile of v0, /device:TPU:0, one launch (start us, length us, event | category | flops | bytes accessed | tf_op | source)
XLA Modules:
  0.0 1631.1 jit_solution(5330102366979640390)
XLA Ops:
  10.5 43.5 %all-reduce.5 = (f32[1536]{0:T(1024)S(1)}, f32[1536]{0:T(1024)S(1)}) all-reduce(f32[1536]{0:T(1024)S(1)} %dynamic-update-slice, f32[1536]{0:T(1024)S(1)} %dynamic-update-slice.1), channel_id=1, replica_groups=mesh['dp'=8,'ctx'=4] {'dp','ctx'}, use_global_device_ids=true, to_apply=%add | all-reduce | flops 3072 | bytes 24576
  57.1 38.7 %all-gather.6.cloned.1.call-done = bf16[3072,1536]{1,0:T(8,128)(2,1)} async-done(((bf16[96,1536]{1,0:T(8,128)(2,1)}), bf16[3072,1536]{1,0:T(8,128)(2,1)}) %all-gather.6.cloned.1.call-update) | async-done | bytes 9437200 | tf_op jit(solution)/shard_map/all_gather | solution.py:105
  95.9 5.5 fusion.44
  111.3 20.5 %all-gather.8.cloned.1.call-done = bf16[1024,1536]{1,0:T(8,128)(2,1)} async-done(((bf16[256,1536]{1,0:T(8,128)(2,1)}), bf16[1024,1536]{1,0:T(8,128)(2,1)}) %all-gather.8.cloned.1.call-update) | async-done | bytes 3145744 | tf_op jit(solution)/shard_map/all_gather | solution.py:150
  136.4 4.3 fusion.17
  144.8 4.1 fusion.35
  148.9 49.5 %all-gather.10.cloned.1.call-done = bf16[1536,1536]{1,0:T(8,128)(2,1)} async-done(((bf16[48,1536]{1,0:T(8,128)(2,1)}), bf16[1536,1536]{1,0:T(8,128)(2,1)}) %all-gather.10.cloned.1.call-update) | async-done | bytes 4718608 | tf_op jit(solution)/shard_map/all_gather | solution.py:106
  202.3 151.2 %all-gather.12.cloned.1.call-done = bf16[8192,1536]{1,0:T(8,128)(2,1)} async-done(((bf16[256,1536]{1,0:T(8,128)(2,1)}), bf16[8192,1536]{1,0:T(8,128)(2,1)}) %all-gather.12.cloned.1.call-update) | async-done | bytes 25165840 | tf_op jit(solution)/shard_map/all_gather | solution.py:173
  353.5 13.7 fusion.66
  367.2 82.5 %all-gather.14.cloned.1.call-done = bf16[1536,4096]{1,0:T(8,128)(2,1)} async-done(((bf16[48,4096]{1,0:T(8,128)(2,1)}), bf16[1536,4096]{1,0:T(8,128)(2,1)}) %all-gather.14.cloned.1.call-update) | async-done | bytes 12582928 | tf_op jit(solution)/shard_map/all_gather | solution.py:174
  449.6 13.2 multiply_convert_fusion.1
  462.9 13.9 multiply_reduce_fusion
  482.3 59.7 %while.15 = (s32[]{:T(128)}, f32[256,8,2,96]{0,3,2,1:T(8,128)}, bf16[2,512,1536]{2,1,0:T(8,128)(2,1)}, s32[2]{0:T(128)S(1)}, bf16[1024,1536]{1,0:T(8,128)(2,1)},...) while((s32[]{:T(128)}, f32[256,8,2,96]{0,3,2,1:T(8,128)}, ...), condition=%wide.region_16.17_spmd.clone, body=%wide.region_13.16_spmd.clone.sunk | while | flops 2043966464 | bytes 114495864 | solution.py:260
  485.5 5.7 fusion.124
  491.9 6.7 fusion.127
  498.6 4.3 bitcast_add_fusion.2
  515.0 5.7 fusion.124
  521.4 6.7 fusion.127
  528.1 4.8 bitcast_add_fusion.2
  542.0 4.6 copy.71
  548.3 6.0 fusion.40
  556.9 26.3 %reduce-scatter.8.cloned.1.call-done = bf16[256,1536]{0,1:T(8,128)(2,1)} async-done(((bf16[1024,1536]{0,1:T(8,128)(2,1)}), bf16[256,1536]{0,1:T(8,128)(2,1)}) %reduce-scatter.8.cloned.1.call-update) | async-done | bytes 786448 | tf_op jit(solution)/shard_map/reduce_scatter | solution.py:265
  585.1 9.6 fusion.38
  594.7 14.9 convolution_bitcast_fusion
  609.6 25.3 %copy.83 = f32[1536,4096]{1,0:T(8,128)} copy(f32[1536,4096]{0,1:T(8,128)} %convolution_bitcast_fusion) | data formatting | bytes 50331648
  635.6 22.7 %fusion.23 = f32[8192,1536]{1,0:T(8,128)} fusion(bf16[256,4096]{1,0:T(8,128)(2,1)} %copy-done.14, bf16[256,4096]{1,0:T(8,128)(2,1)} %copy-done.13, f32[256,1536]{1,0:T(8,128)} %copy-done.6, f32[1536]{0:T(1024)S(1)} %copy-done.25, f32[256]{0:T(256)} %copy-done.30), kind=kOutput, calls=%fused_computation.54 | convolution fusion | flops 6452019200 | bytes 56105984 | tf_op jit(solution)/shard_map/dot_general | solution.py:193
  658.4 10.2 fusion.25
  668.6 8.5 fusion.34
  677.1 41.0 %all-reduce.4 = (f32[1536]{0:T(1024)S(1)}, f32[1536]{0:T(1024)S(1)}) all-reduce(f32[1536]{0:T(1024)} %get-tuple-element.305, f32[1536]{0:T(1024)} %get-tuple-element.303), channel_id=3, replica_groups=mesh['dp'=8,'ctx'=4] {'dp','ctx'}, use_global_device_ids=true, to_apply=%region_20.21.clone | all-reduce | flops 3072 | bytes 24576
  726.3 212.8 %reduce-scatter.10.cloned.1.call-done = f32[96,1536]{1,0:T(8,128)} async-done(((f32[3072,1536]{1,0:T(8,128)}), f32[96,1536]{1,0:T(8,128)}) %reduce-scatter.10.cloned.1.call-update) | async-done | bytes 589840 | tf_op jit(solution)/shard_map/reduce_scatter | solution.py:82
  939.1 249.2 %reduce-scatter.16.cloned.1.call-done = f32[48,4096]{1,0:T(8,128)} async-done(((f32[1536,4096]{1,0:T(8,128)}), f32[48,4096]{1,0:T(8,128)}) %reduce-scatter.16.cloned.1.call-update) | async-done | bytes 786448
  1188.3 435.5 %reduce-scatter.14.cloned.1.call-done = f32[256,1536]{1,0:T(8,128)} async-done(((f32[8192,1536]{1,0:T(8,128)}), f32[256,1536]{1,0:T(8,128)}) %reduce-scatter.14.cloned.1.call-update) | async-done | bytes 1572880 | tf_op jit(solution)/shard_map/reduce_scatter | solution.py:82
  (181 shorter events, 73.4 us)
Async XLA Ops:
  7.2 88.7 %all-gather.6.cloned.1.call-start = ((), (), s32[]{:S(2)}) async-start(), calls=%async_computation.5 | async-start | bytes 9732096 | tf_op jit(solution)/shard_map/all_gather | solution.py:105
  7.9 124.0 %all-gather.8.cloned.1.call-start = ((), (), s32[]{:S(2)}) async-start(), calls=%async_computation.6 | async-start | bytes 3932160 | tf_op jit(solution)/shard_map/all_gather | solution.py:150
  54.0 47.3 %copy-start.22 = (f32[1536]{0:T(1024)}, f32[1536]{0:T(1024)S(1)}, u32[]{:S(2)}) copy-start(f32[1536]{0:T(1024)S(1)} %get-tuple-element.337) | copy-start | bytes 18436
  54.0 422.7 %copy-start.24 = (f32[1536]{0:T(1024)}, f32[1536]{0:T(1024)S(1)}, u32[]{:S(2)}) copy-start(f32[1536]{0:T(1024)S(1)} %get-tuple-element.338) | copy-start | bytes 18436
  56.8 44.5 %copy-start.27 = (f32[256]{0:T(256)}, f32[256]{0:T(256)S(1)}, u32[]{:S(2)}) copy-start(f32[256]{0:T(256)S(1)} %get-tuple-element.359) | copy-start | bytes 3076
  57.1 52.8 %copy-start.18 = (f32[256,48]{0,1:T(8,128)}, f32[256,48]{0,1:T(8,128)S(1)}, u32[]{:S(2)}) copy-start(f32[256,48]{0,1:T(8,128)S(1)} %get-tuple-element.356) | copy-start | bytes 147460
  57.1 52.8 %copy-start.20 = (f32[256,48]{0,1:T(8,128)}, f32[256,48]{0,1:T(8,128)S(1)}, u32[]{:S(2)}) copy-start(f32[256,48]{0,1:T(8,128)S(1)} %get-tuple-element.357) | copy-start | bytes 147460
  104.7 93.7 %all-gather.10.cloned.1.call-start = ((), (), s32[]{:S(2)}) async-start(), calls=%async_computation.7 | async-start | bytes 4866048 | tf_op jit(solution)/shard_map/all_gather | solution.py:106
  105.4 248.1 %all-gather.12.cloned.1.call-start = ((), (), s32[]{:S(2)}) async-start(), calls=%async_computation.8 | async-start | bytes 25952256 | tf_op jit(solution)/shard_map/all_gather | solution.py:173
  106.0 343.6 %all-gather.14.cloned.1.call-start = ((), (), s32[]{:S(2)}) async-start(), calls=%async_computation.9 | async-start | bytes 12976128 | tf_op jit(solution)/shard_map/all_gather | solution.py:174
  106.6 476.6 %reduce-scatter.8.cloned.1.call-start = ((), (), s32[]{:S(2)}) async-start(), calls=%async_computation.10 | async-start | bytes 3932160 | tf_op jit(solution)/shard_map/reduce_scatter | solution.py:265
  144.8 53.6 %copy-start.4 = (bf16[256,1536]{1,0:T(8,128)(2,1)S(1)}, bf16[256,1536]{1,0:T(8,128)(2,1)}, u32[]{:S(2)}) copy-start(bf16[256,1536]{1,0:T(8,128)(2,1)} %param.12) | copy-start | bytes 2359300
  148.9 332.0 %copy-start.9 = (bf16[256,8,2,96]{0,3,2,1:T(8,128)(2,1)}, bf16[256,8,2,96]{0,3,2,1:T(8,128)(2,1)S(1)}, u32[]{:S(2)}) copy-start(bf16[256,8,2,96]{0,3,2,1:T(8,128)(2,1)S(1)} %fusion.35) | copy-start | bytes 2359300
  202.2 274.5 %copy-start.6 = (f32[256,1536]{1,0:T(8,128)}, f32[256,1536]{1,0:T(8,128)S(1)}, u32[]{:S(2)}) copy-start(f32[256,1536]{1,0:T(8,128)S(1)} %get-tuple-element.365) | copy-start | bytes 4718596
  202.3 274.5 %copy-start.30 = (f32[256]{0:T(256)}, f32[256]{0:T(256)S(1)}, u32[]{:S(2)}) copy-start(f32[256]{0:T(256)S(1)} %get-tuple-element.361) | copy-start | bytes 3076
  353.5 96.1 %copy-start.11 = (bf16[256,1536]{1,0:T(8,128)(2,1)S(1)}, bf16[256,1536]{1,0:T(8,128)(2,1)}, u32[]{:S(2)}) copy-start(bf16[256,1536]{1,0:T(8,128)(2,1)} %param.19) | copy-start | bytes 2359300
  449.6 28.7 %slice-start = ((s8[4718592]{0:T(1024)(128)(4,1)}), s8[4194304]{0:T(1024)(128)(4,1)S(1)}, s32[]{:S(2)}) async-start(s8[4718592]{0:T(1024)(128)(4,1)} %bitcast.195), calls=%async_computation.15 | async-start | bytes 8388608
  462.9 13.9 copy-start.13
  462.9 13.9 copy-start.14
  462.9 15.5 slice-start.1
  498.6 5.2 copy-start.1
  528.1 5.7 copy-start.1
  546.7 179.6 %reduce-scatter.12.cloned.1.call-start = ((), (), s32[]{:S(2)}) async-start(), calls=%async_computation.12 | async-start | bytes 9732096 | tf_op jit(solution)/shard_map/reduce_scatter | solution.py:83
  554.3 384.8 %reduce-scatter.10.cloned.1.call-start = ((), (), s32[]{:S(2)}) async-start(), calls=%async_computation.11 | async-start | bytes 19464192 | tf_op jit(solution)/shard_map/reduce_scatter | solution.py:82
  556.8 28.3 %copy-start.5 = (bf16[256,1536]{1,0:T(8,128)(2,1)S(1)}, bf16[256,1536]{1,0:T(8,128)(2,1)}, u32[]{:S(2)}) copy-start(bf16[256,1536]{1,0:T(8,128)(2,1)} %param.12) | copy-start | bytes 2359300
  556.8 28.2 %copy-start.23 = (f32[1536]{0:T(1024)S(1)}, f32[1536]{0:T(1024)}, u32[]{:S(2)}) copy-start(f32[1536]{0:T(1024)} %copy-done.22) | copy-start | bytes 18436
  556.9 28.2 %copy-start.28 = (f32[256]{0:T(256)S(1)}, f32[256]{0:T(256)}, u32[]{:S(2)}) copy-start(f32[256]{0:T(256)} %copy-done.27) | copy-start | bytes 3076
  594.7 593.6 %reduce-scatter.16.cloned.1.call-start = ((), (), s32[]{:S(2)}) async-start(), calls=%async_computation.14 | async-start | bytes 25952256
  635.0 988.9 %reduce-scatter.14.cloned.1.call-start = ((), (), s32[]{:S(2)}) async-start(), calls=%async_computation.13 | async-start | bytes 51904512 | tf_op jit(solution)/shard_map/reduce_scatter | solution.py:82
  658.4 10.2 copy-start.17
  658.4 10.2 copy-start.29
  668.6 51.4 %copy-start.31 = (f32[256]{0:T(256)S(1)}, f32[256]{0:T(256)}, u32[]{:S(2)}) copy-start(f32[256]{0:T(256)} %get-tuple-element.358) | copy-start | bytes 3076
  (15 other events, 29.9 us)
Sparse Core Ops, SparseCore 0:
  10.9 84.9 all-gather.5
  104.8 27.0 all-gather.7
  134.8 63.5 all-gather.9
  201.1 152.3 all-gather.11
  356.2 93.3 all-gather.13
  546.8 36.2 reduce-scatter.7
  589.6 136.6 reduce-scatter.11
  733.3 205.7 reduce-scatter.9
  946.1 242.1 reduce-scatter.15
  1195.1 428.6 reduce-scatter.13
where the time goes:
time: 1640 us; the launch traced here: 1630 us
  waiting for transfers between devices  1270 us (77%)
  matrix products  178 us (11%)
  blocking collectives  84.6 us (5%)
  local copies, waits for them, and re-layouts  59.6 us (4%)
  other arithmetic  19.4 us (1%)
    reduce_scatter x2, waiting for transfers between devices, owned_three(): lax.psum_scatter(second_part, ('dp', 'ctx'), scatter_dimension=0, tiled=T...  648 us
    unnamed x11, waiting for transfers between devices  252 us
    all_gather x1, waiting for transfers between devices, shards(): lax.all_gather(w_gate_up, ('dp', 'ctx'), axis=0, tiled=True)  151 us
    unnamed x2, blocking collectives  84.6 us
    all_gather x1, waiting for transfers between devices, shards(): lax.all_gather(w_down, ('dp', 'ctx'), axis=0, tiled=True)  82.5 us
    all_gather x1, waiting for transfers between devices, shards(): lax.all_gather(w_out, ('dp', 'ctx'), axis=0, tiled=True)  49.5 us
    all_gather x1, waiting for transfers between devices, shards(): lax.all_gather(w_qkv, ('dp', 'ctx'), axis=0, tiled=True)  38.7 us
    dot_general x4, matrix products, full_back(): return jnp.dot(grad_side, whole_weight, preferred_element_type=jnp.float32)  37 us
  transfers between devices with their start and end apart: 10, of which 10 were waited for; matrix products, arithmetic and copies ran while one was open for 9% of the time, Pallas kernels for 0%

commit v1 on v0

--- a/solution.py
+++ b/solution.py
@@ -1,3 +1,4 @@
+import functools
 import math
 import jax
 import jax.numpy as jnp
@@ -14,6 +15,18 @@
 EPSILON = 1e-05
 THETA = 100000.0
 MASK_FILL = -1e30
+
+
+def fill_blocks_all(arr_in, axis_id):
+    total_devices = jax.lax.axis_size(axis_id)
+    copies = tuple((total_devices if dev_j == 0 else 1 for dev_j in range(arr_in.ndim)))
+    fresh = jax.lax.all_to_all(
+        jnp.tile(arr_in, copies), axis_id, split_axis=0, concat_axis=0, tiled=True
+    )
+    return fresh
+
+
+finish_run_now = functools.partial(fill_blocks_all, axis_id=("dp", "ctx"))
 
 
 def rope_tables(rope_pos):
@@ -170,7 +183,7 @@
     scale_two = lax.rsqrt(jnp.mean(residual * residual, -1, keepdims=True) + EPSILON)
     normed_two = (residual * scale_two * gain_two).astype(jnp.bfloat16)
     gate_up_full, down_full = (
-        lax.all_gather(w_gate_up, ("dp", "ctx"), axis=0, tiled=True),
+        finish_run_now(w_gate_up),
         lax.all_gather(w_down, ("dp", "ctx"), axis=0, tiled=True),
     )
     gate_up = full_product(normed_two, gate_up_full)

time: 1640 us -> 2080 us (1.27)
  waiting for transfers between devices: 1270 us -> 1700 us
    all_to_all x0 -> x1, waiting for transfers between devices: none -> 438 us  [fill_blocks_all(): jax.lax.all_to_all(jnp.tile(arr_in, copies), axis_id, split_axis=0, conca...]
    all_gather x1, waiting for transfers between devices: 49.5 us -> 243 us  [shards(): lax.all_gather(w_out, ('dp', 'ctx'), axis=0, tiled=True)]
    all_gather x1, waiting for transfers between devices: 151 us -> 0.01 us  [shards(): lax.all_gather(w_gate_up, ('dp', 'ctx'), axis=0, tiled=True)]
    all_gather x1, waiting for transfers between devices: 82.5 us -> 0.01 us  [shards(): lax.all_gather(w_down, ('dp', 'ctx'), axis=0, tiled=True)]
  transfers between devices with their start and end apart: 10 -> 11, of which waited for: 10 -> 9; matrix products, arithmetic and copies ran while one was open for 9% -> 8% of each run, Pallas kernels for 0% -> 0%
where the time goes in v1:
time: 2080 us
  waiting for transfers between devices  1700 us (82%)
  matrix products  180 us (9%)
  blocking collectives  84.5 us (4%)
  local copies, waits for them, and re-layouts  68.7 us (3%)
    reduce_scatter x2, waiting for transfers between devices, owned_three(): lax.psum_scatter(second_part, ('dp', 'ctx'), scatter_dimension=0, tiled=T...  648 us
    all_to_all x1, waiting for transfers between devices, fill_blocks_all(): jax.lax.all_to_all(jnp.tile(arr_in, copies), axis_id, split_axis=0, conca...  438 us
    unnamed x11, waiting for transfers between devices  252 us
    all_gather x1, waiting for transfers between devices, shards(): lax.all_gather(w_out, ('dp', 'ctx'), axis=0, tiled=True)  243 us
    unnamed x2, blocking collectives  84.5 us
    reduce_scatter x1, waiting for transfers between devices, shards(): lax.psum_scatter(key_terms.reshape(grouped_rows, 2 * KEY_FEATURES).astype...  46.7 us
  transfers between devices with their start and end apart: 11, of which 9 were waited for; matrix products, arithmetic and copies ran while one was open for 8% of the time, Pallas kernels for 0%

profile of v1, /device:TPU:0, one launch (start us, length us, event | category | flops | bytes accessed | tf_op | source)
XLA Modules:
  0.0 2077.1 jit_solution(1028406205708396951)
XLA Ops:
  10.5 43.5 %all-reduce.5 = (f32[1536]{0:T(1024)S(1)}, f32[1536]{0:T(1024)S(1)}) all-reduce(f32[1536]{0:T(1024)S(1)} %dynamic-update-slice, f32[1536]{0:T(1024)S(1)} %dynamic-update-slice.1), channel_id=1, replica_groups=mesh['dp'=8,'ctx'=4] {'dp','ctx'}, use_global_device_ids=true, to_apply=%add | all-reduce | flops 3072 | bytes 24576
  57.2 38.7 %all-gather.6.cloned.1.call-done = bf16[3072,1536]{1,0:T(8,128)(2,1)} async-done(((bf16[96,1536]{1,0:T(8,128)(2,1)}), bf16[3072,1536]{1,0:T(8,128)(2,1)}) %all-gather.6.cloned.1.call-update) | async-done | bytes 9437200 | tf_op jit(solution)/shard_map/all_gather | solution.py:118
  95.8 5.5 fusion.44
  106.0 9.1 tile.2
  115.0 4.3 all-to-all-start
  124.6 33.7 %all-gather.8.cloned.1.call-done = bf16[1024,1536]{1,0:T(8,128)(2,1)} async-done(((bf16[256,1536]{1,0:T(8,128)(2,1)}), bf16[1024,1536]{1,0:T(8,128)(2,1)}) %all-gather.8.cloned.1.call-update) | async-done | bytes 3145744 | tf_op jit(solution)/shard_map/all_gather | solution.py:163
  162.7 4.3 fusion.17
  175.3 242.8 %all-gather.10.cloned.1.call-done = bf16[1536,1536]{1,0:T(8,128)(2,1)} async-done(((bf16[48,1536]{1,0:T(8,128)(2,1)}), bf16[1536,1536]{1,0:T(8,128)(2,1)}) %all-gather.10.cloned.1.call-update) | async-done | bytes 4718608 | tf_op jit(solution)/shard_map/all_gather | solution.py:119
  421.9 437.6 %all-to-all-done = bf16[32,256,1536]{2,1,0:T(8,128)(2,1)} async-done(((bf16[32,256,1536]{2,1,0:T(8,128)(2,1)}), bf16[32,256,1536]{2,1,0:T(8,128)(2,1)}, u32[]{:S(2)}, u32[]{:S(2)}) %all-to-all-start) | async-done | bytes 25165856 | tf_op jit(solution)/shard_map/all_to_all | solution.py:23
  859.5 14.1 fusion.66
  873.6 13.7 multiply_convert_fusion.1
  887.3 13.6 multiply_reduce_fusion
  908.8 59.8 %while.15 = (s32[]{:T(128)}, f32[256,8,2,96]{0,3,2,1:T(8,128)}, bf16[2,512,1536]{2,1,0:T(8,128)(2,1)}, s32[2]{0:T(128)S(1)}, bf16[1024,1536]{1,0:T(8,128)(2,1)},...) while((s32[]{:T(128)}, f32[256,8,2,96]{0,3,2,1:T(8,128)}, ...), condition=%wide.region_16.17_spmd.clone, body=%wide.region_13.16_spmd.clone.sunk | while | flops 2043966464 | bytes 114495864 | solution.py:273
  912.0 5.7 fusion.124
  918.4 6.7 fusion.127
  925.1 4.3 bitcast_add_fusion.2
  941.6 5.7 fusion.124
  947.9 6.7 fusion.127
  954.6 4.8 bitcast_add_fusion.2
  968.6 4.6 copy.71
  974.9 5.1 fusion.40
  982.4 46.7 %reduce-scatter.8.cloned.1.call-done = bf16[256,1536]{0,1:T(8,128)(2,1)} async-done(((bf16[1024,1536]{0,1:T(8,128)(2,1)}), bf16[256,1536]{0,1:T(8,128)(2,1)}) %reduce-scatter.8.cloned.1.call-update) | async-done | bytes 786448 | tf_op jit(solution)/shard_map/reduce_scatter | solution.py:278
  1031.1 9.6 fusion.38
  1040.7 14.9 convolution_bitcast_fusion
  1055.6 25.4 %copy.83 = f32[1536,4096]{1,0:T(8,128)} copy(f32[1536,4096]{0,1:T(8,128)} %convolution_bitcast_fusion) | data formatting | bytes 50331648
  1081.7 22.7 %fusion.23 = f32[8192,1536]{1,0:T(8,128)} fusion(bf16[256,4096]{1,0:T(8,128)(2,1)} %get-tuple-element.342, bf16[256,4096]{1,0:T(8,128)(2,1)} %get-tuple-element.341, f32[256,1536]{1,0:T(8,128)} %copy-done.6, f32[1536]{0:T(1024)S(1)} %copy-done.24, f32[256]{0:T(256)} %copy-done.29), kind=kOutput, calls=%fused_computation.54 | convolution fusion | flops 6452019200 | bytes 56105984 | tf_op jit(solution)/shard_map/dot_general | solution.py:206
  1104.5 10.2 fusion.25
  1114.6 8.5 fusion.34
  1123.2 41.0 %all-reduce.4 = (f32[1536]{0:T(1024)S(1)}, f32[1536]{0:T(1024)S(1)}) all-reduce(f32[1536]{0:T(1024)} %get-tuple-element.305, f32[1536]{0:T(1024)} %get-tuple-element.303), channel_id=3, replica_groups=mesh['dp'=8,'ctx'=4] {'dp','ctx'}, use_global_device_ids=true, to_apply=%region_20.21.clone | all-reduce | flops 3072 | bytes 24576
  1172.3 212.8 %reduce-scatter.10.cloned.1.call-done = f32[96,1536]{1,0:T(8,128)} async-done(((f32[3072,1536]{1,0:T(8,128)}), f32[96,1536]{1,0:T(8,128)}) %reduce-scatter.10.cloned.1.call-update) | async-done | bytes 589840 | tf_op jit(solution)/shard_map/reduce_scatter | solution.py:95
  1385.1 249.1 %reduce-scatter.16.cloned.1.call-done = f32[48,4096]{1,0:T(8,128)} async-done(((f32[1536,4096]{1,0:T(8,128)}), f32[48,4096]{1,0:T(8,128)}) %reduce-scatter.16.cloned.1.call-update) | async-done | bytes 786448
  1634.2 435.6 %reduce-scatter.14.cloned.1.call-done = f32[256,1536]{1,0:T(8,128)} async-done(((f32[8192,1536]{1,0:T(8,128)}), f32[256,1536]{1,0:T(8,128)}) %reduce-scatter.14.cloned.1.call-update) | async-done | bytes 1572880 | tf_op jit(solution)/shard_map/reduce_scatter | solution.py:95
  (177 shorter events, 79.7 us)
Async XLA Ops:
  7.2 88.6 %all-gather.6.cloned.1.call-start = ((), (), s32[]{:S(2)}) async-start(), calls=%async_computation.6 | async-start | bytes 9732096 | tf_op jit(solution)/shard_map/all_gather | solution.py:118
  7.9 150.3 %all-gather.8.cloned.1.call-start = ((), (), s32[]{:S(2)}) async-start(), calls=%async_computation.7 | async-start | bytes 3932160 | tf_op jit(solution)/shard_map/all_gather | solution.py:163
  54.0 47.2 %copy-start.21 = (f32[1536]{0:T(1024)}, f32[1536]{0:T(1024)S(1)}, u32[]{:S(2)}) copy-start(f32[1536]{0:T(1024)S(1)} %get-tuple-element.337) | copy-start | bytes 18436
  54.0 846.9 %copy-start.23 = (f32[1536]{0:T(1024)}, f32[1536]{0:T(1024)S(1)}, u32[]{:S(2)}) copy-start(f32[1536]{0:T(1024)S(1)} %get-tuple-element.338) | copy-start | bytes 18436
  56.9 44.4 %copy-start.26 = (f32[256]{0:T(256)}, f32[256]{0:T(256)S(1)}, u32[]{:S(2)}) copy-start(f32[256]{0:T(256)S(1)} %get-tuple-element.359) | copy-start | bytes 3076
  57.1 66.1 %copy-start.17 = (f32[256,48]{0,1:T(8,128)}, f32[256,48]{0,1:T(8,128)S(1)}, u32[]{:S(2)}) copy-start(f32[256,48]{0,1:T(8,128)S(1)} %get-tuple-element.356) | copy-start | bytes 147460
  57.1 66.1 %copy-start.19 = (f32[256,48]{0,1:T(8,128)}, f32[256,48]{0,1:T(8,128)S(1)}, u32[]{:S(2)}) copy-start(f32[256,48]{0,1:T(8,128)S(1)} %get-tuple-element.357) | copy-start | bytes 147460
  104.6 313.4 %all-gather.10.cloned.1.call-start = ((), (), s32[]{:S(2)}) async-start(), calls=%async_computation.8 | async-start | bytes 4866048 | tf_op jit(solution)/shard_map/all_gather | solution.py:119
  105.4 768.2 %all-gather.12.cloned.1.call-start = ((), (), s32[]{:S(2)}) async-start(), calls=%async_computation.9 | async-start | bytes 12976128 | tf_op jit(solution)/shard_map/all_gather | solution.py:187
  115.0 5.5 copy-start.31
  115.0 5.6 copy-start.25
  115.0 744.5 %all-to-all-start = ((bf16[32,256,1536]{2,1,0:T(8,128)(2,1)}), bf16[32,256,1536]{2,1,0:T(8,128)(2,1)}, u32[]{:S(2)}, u32[]{:S(2)}) async-start(bf16[32,256,1536]{2,1,0:T(8,128)(2,1)} %tile.2), calls=%async_computation | async-start | bytes 50331648 | tf_op jit(solution)/shard_map/all_to_all | solution.py:23
  119.3 768.0 %all-gather.14.cloned.1.call-start = ((), (), s32[]{:S(2)}) async-start(), calls=%async_computation.10 | async-start | bytes 25952256 | tf_op jit(solution)/shard_map/all_gather | solution.py:197
  119.9 909.3 %reduce-scatter.8.cloned.1.call-start = ((), (), s32[]{:S(2)}) async-start(), calls=%async_computation.11 | async-start | bytes 3932160 | tf_op jit(solution)/shard_map/reduce_scatter | solution.py:278
  167.1 4.1 copy-start.14
  171.1 246.9 %copy-start.4 = (bf16[256,1536]{1,0:T(8,128)(2,1)S(1)}, bf16[256,1536]{1,0:T(8,128)(2,1)}, u32[]{:S(2)}) copy-start(bf16[256,1536]{1,0:T(8,128)(2,1)} %param.12) | copy-start | bytes 2359300
  175.2 732.1 %copy-start.10 = (bf16[256,8,2,96]{0,3,2,1:T(8,128)(2,1)}, bf16[256,8,2,96]{0,3,2,1:T(8,128)(2,1)S(1)}, u32[]{:S(2)}) copy-start(bf16[256,8,2,96]{0,3,2,1:T(8,128)(2,1)S(1)} %fusion.35) | copy-start | bytes 2359300
  421.9 479.0 %copy-start.6 = (f32[256,1536]{1,0:T(8,128)}, f32[256,1536]{1,0:T(8,128)S(1)}, u32[]{:S(2)}) copy-start(f32[256,1536]{1,0:T(8,128)S(1)} %get-tuple-element.365) | copy-start | bytes 4718596
  421.9 479.0 %copy-start.29 = (f32[256]{0:T(256)}, f32[256]{0:T(256)S(1)}, u32[]{:S(2)}) copy-start(f32[256]{0:T(256)S(1)} %get-tuple-element.361) | copy-start | bytes 3076
  859.5 14.1 copy-start.12
  925.1 5.2 copy-start.1
  954.6 5.7 copy-start.1
  973.3 199.0 %reduce-scatter.12.cloned.1.call-start = ((), (), s32[]{:S(2)}) async-start(), calls=%async_computation.13 | async-start | bytes 9732096 | tf_op jit(solution)/shard_map/reduce_scatter | solution.py:96
  980.0 405.1 %reduce-scatter.10.cloned.1.call-start = ((), (), s32[]{:S(2)}) async-start(), calls=%async_computation.12 | async-start | bytes 19464192 | tf_op jit(solution)/shard_map/reduce_scatter | solution.py:95
  982.4 48.7 %copy-start.5 = (bf16[256,1536]{1,0:T(8,128)(2,1)S(1)}, bf16[256,1536]{1,0:T(8,128)(2,1)}, u32[]{:S(2)}) copy-start(bf16[256,1536]{1,0:T(8,128)(2,1)} %param.12) | copy-start | bytes 2359300
  982.4 48.7 %copy-start.22 = (f32[1536]{0:T(1024)S(1)}, f32[1536]{0:T(1024)}, u32[]{:S(2)}) copy-start(f32[1536]{0:T(1024)} %copy-done.21) | copy-start | bytes 18436
  982.4 48.7 %copy-start.27 = (f32[256]{0:T(256)S(1)}, f32[256]{0:T(256)}, u32[]{:S(2)}) copy-start(f32[256]{0:T(256)} %copy-done.26) | copy-start | bytes 3076
  1040.7 593.5 %reduce-scatter.16.cloned.1.call-start = ((), (), s32[]{:S(2)}) async-start(), calls=%async_computation.15 | async-start | bytes 25952256
  1081.0 988.8 %reduce-scatter.14.cloned.1.call-start = ((), (), s32[]{:S(2)}) async-start(), calls=%async_computation.14 | async-start | bytes 51904512 | tf_op jit(solution)/shard_map/reduce_scatter | solution.py:95
  1104.4 10.2 copy-start.16
  1104.4 10.2 copy-start.28
  1114.6 51.4 %copy-start.30 = (f32[256]{0:T(256)S(1)}, f32[256]{0:T(256)}, u32[]{:S(2)}) copy-start(f32[256]{0:T(256)} %get-tuple-element.358) | copy-start | bytes 3076
  (13 other events, 20.9 us)
Sparse Core Ops, SparseCore 0:
  10.9 84.8 all-gather.5
  104.8 53.4 all-gather.7
  161.2 256.8 all-gather.9
  420.8 211.0 all-gather.11
  634.6 239.3 all-gather.13
  973.4 55.7 reduce-scatter.7
  1035.6 136.6 reduce-scatter.11
  1179.3 205.7 reduce-scatter.9
  1392.1 242.0 reduce-scatter.15
  1641.1 428.6 reduce-scatter.13
